TPU v7x, 512 devices: a whole 4x8x8 slice. The times are simulated.
512 devices in a mesh: row: 32 (over x, y), col: 16 (over z, core).
Axes of the slice: x: 4, y: 8, z: 8, core: 2. Of those that a mesh axis runs over, the one named last changes fastest.
Arguments:
- inverse_block: float32 [16384, 16384], P('row', 'col'), may hold values from -6 to 6
- tile_list: int32 [32], replicated, may hold values from 0 to 63, as said below
- panels: bfloat16 [3, 16384, 512], P(None, 'row'), may hold values from -0.0625 to 0.0625
- links: bfloat16 [2, 512, 512], P(None, 'col'), may hold values from -0.25 to 0.25
- diag_inverse: float32 [3, 512, 512], P(None, None, 'col'), may hold values from -6 to 6
Outputs:
- panel_inverse: float32 [3, 16384, 512], P(None, 'row', 'col')
- cross_inverse: float32 [2, 512, 512], P(None, None, 'col')
- diag_block: float32 [3, 512, 512], P(None, None, 'col')
Inputs may be any that keep to these rules, and one draw needn't show every extreme that they name: `tile_list`: 32 different tile numbers in ascending order; for each g from 0 to 16 - 1, the aligned group of tiles g * (64 // 16) to (g + 1) * (64 // 16) - 1 holds at least one of them.
All inputs are finite; a program needn't handle non-finite values.
Results may differ from a plain program's by a relative error of at most 0.0003.
Values may be sent and summed in bfloat16 or wider, within the bound.
A program may use at most 64 MiB of HBM per device.

v0:
```python
import jax
import jax.numpy as jnp
from jax import lax
from jax.sharding import Mesh
from jax.sharding import PartitionSpec as P

ORDER = 16384
TILE = 256
ROW = ("row_0", "row_1")
precise = lax.Precision.HIGHEST


def from_root(array, axes, root):
    array = jnp.where(lax.axis_index(axes) == root, array, jnp.zeros_like(array))
    for axis in axes:
        array = lax.psum(array, axis)
    return array


def laid_out(blocks, dim):
    blocks = jnp.moveaxis(blocks, 0, dim)
    shape = blocks.shape
    return blocks.reshape(*shape[:dim], shape[dim] * shape[dim + 1], *shape[dim + 2 :])


def copy_for_each(array, axis):
    copies = jnp.broadcast_to(array, (lax.axis_size(axis), *array.shape))
    return lax.all_to_all(copies, axis, split_axis=0, concat_axis=0, tiled=True)


def gathered_copies(array, axis, dim):
    return laid_out(copy_for_each(array, axis), dim)


def split_up(array, dim, peers):
    shape = array.shape
    blocks = array.reshape(*shape[:dim], peers, shape[dim] // peers, *shape[dim + 1 :])
    return jnp.moveaxis(blocks, dim, 0)


def sent_and_summed(array, axis, dim):
    blocks = split_up(array, dim, lax.axis_size(axis))
    arrived = lax.all_to_all(blocks, axis, split_axis=0, concat_axis=0, tiled=True)
    return arrived.sum(axis=0)


def of_everyone(array, axis):
    everything = copy_for_each(array, axis)
    return jnp.sum(everything, axis=0)


def rows_for(lines, peers):
    spare = -len(lines) % peers
    return jnp.pad(lines, [(0, spare)] + [(0, 0)] * (lines.ndim - 1))


def total_of(array, axes):
    own = sent_and_summed(rows_for(array, lax.axis_size(axes)), axes, 0)
    whole = gathered_copies(own, axes, 0)
    return whole[: len(array)].reshape(array.shape)


def together(arrays, axis):
    ravelled, at, gathered = (jnp.concatenate([a.reshape(-1) for a in arrays]), 0, [])
    subtotal = total_of(ravelled, axis)
    for a in arrays:
        gathered.append(subtotal[at : at + a.size].reshape(a.shape))
        at += a.size
    return tuple(gathered)


def product(left, right):
    return jnp.dot(left, right, precision=precise, preferred_element_type=jnp.float32)


def local(inverse_block, tile_list, panels, links, diag_inverse):
    rows_here = inverse_block.shape[0]
    width_here = diag_inverse.shape[2]
    ratio = lax.axis_size(ROW) // lax.axis_size("col")
    row_number = lax.axis_index(ROW)
    col_number = lax.axis_index("col")
    tile_count = ORDER // TILE
    listed = jnp.any(
        tile_list[:, None] == jnp.arange(tile_count, dtype=jnp.int32)[None, :], axis=0
    ).astype(jnp.float32)
    tiles_here = rows_here // TILE
    mine = lax.dynamic_slice_in_dim(listed, row_number * tiles_here, tiles_here)
    row_mask = jnp.broadcast_to(mine[:, None], (tiles_here, TILE)).reshape(-1)
    supernodes = panels.shape[0]
    panel_parts = []
    cross_parts = []
    diag_parts = []
    previous = None
    diag_prev = None
    for supernode in range(supernodes):
        masked_panel = panels[supernode] * row_mask[:, None].astype(jnp.bfloat16)
        pieces = []
        for source in range(ratio):
            pieces.append(from_root(masked_panel, ROW, col_number * ratio + source))
        column_factor = jnp.concatenate(pieces, axis=0).astype(jnp.float32)
        local_factor = masked_panel.astype(jnp.float32)
        partial_rows = product(inverse_block, column_factor)
        if supernode > 0:
            link_block = gathered_copies(links[supernode - 1], "col", 0).astype(jnp.float32)
            link_share = lax.dynamic_slice_in_dim(
                link_block, col_number * width_here, width_here, 1
            )
            diag_full = lax.all_gather(diag_prev, "col", axis=1, tiled=True)
            factor_share = lax.dynamic_slice_in_dim(
                local_factor, col_number * width_here, width_here, 1
            )
            cross_term = product(previous.T, factor_share)
            carried = product(diag_full, link_share)
        current = sent_and_summed(partial_rows, "col", 1)
        if supernode > 0:
            current = current + product(previous, link_share)
        current = -current * row_mask[:, None]
        if supernode + 1 < supernodes:
            current_full = lax.all_gather(current, "col", axis=1, tiled=True)
        own_term = product(local_factor.T, current)
        if supernode == 0:
            diag_now = diag_inverse[supernode] - of_everyone(own_term, ROW)
        else:
            cross_sum, rest_sum = together(
                (cross_term, own_term - product(link_block.T, cross_term)), ROW
            )
            cross_block = -(cross_sum + carried)
            diag_now = diag_inverse[supernode] - rest_sum + product(link_block.T, carried)
        if supernode > 0:
            cross_parts.append(cross_block)
        panel_parts.append(current)
        diag_parts.append(diag_now)
        if supernode + 1 < supernodes:
            previous = current_full
        diag_prev = diag_now
    return (jnp.stack(panel_parts), jnp.stack(cross_parts), jnp.stack(diag_parts))


def solution(mesh):
    split = Mesh(mesh.devices.reshape(4, 8, mesh.shape["col"]), ("row_0", "row_1", "col"))
    return jax.shard_map(
        local,
        mesh=split,
        in_specs=(
            P(ROW, "col"),
            P(),
            P(None, ROW, None),
            P(None, "col", None),
            P(None, None, "col"),
        ),
        out_specs=(P(None, ROW, "col"), P(None, None, "col"), P(None, None, "col")),
        check_vma=False,
    )
```

profile of v0, /device:TPU:8, one launch (start us, length us, event | category | flops | bytes accessed | tf_op | source)
XLA Modules:
  0.0 482.6 jit_solution(13430602291217242635)
XLA Ops:
  13.2 91.2 %all-reduce.7.cloned.1.call-done = (bf16[512,512]{1,0:T(8,128)(2,1)}, bf16[512,512]{1,0:T(8,128)(2,1)}, bf16[512,512]{1,0:T(8,128)(2,1)}, bf16[512,512]{1,0:T(8,...) async-done(((bf16[512,512]{1,0:T(8,128)(2,1)}, bf16[512,512]{1,0:T(8,128)(2,1)}, bf16[512,512]{1,0:T(8,128)(2,1)}, bf16[512,512]{1,0:T(8,128)(2,1)}, ...) | async-done | bytes 3145744 | tf_op jit(solution)/shard_map/psum | solution.py:16
  105.9 7.5 %all-to-all-start.2 = ((bf16[16,32,512]{2,1,0:T(8,128)(2,1)}), bf16[16,32,512]{2,1,0:T(8,128)(2,1)S(1)}, u32[]{:S(2)}, u32[]{:S(2)}) async-start(bf16[16,32,512]{2,1,0:T(8,128)(2,1)} %broadcast_in_dim.24), calls=%async_computation.2 | async-start | bytes 1048576 | tf_op jit(solution)/shard_map/all_to_all | solution.py:28
  113.4 90.5 %all-reduce.5.cloned.1.call-done = (bf16[512,512]{1,0:T(8,128)(2,1)}, bf16[512,512]{1,0:T(8,128)(2,1)}, bf16[512,512]{1,0:T(8,128)(2,1)}, bf16[512,512]{1,0:T(8,...) async-done(((bf16[512,512]{1,0:T(8,128)(2,1)}, bf16[512,512]{1,0:T(8,128)(2,1)}, bf16[512,512]{1,0:T(8,128)(2,1)}, bf16[512,512]{1,0:T(8,128)(2,1)}, ...) | async-done | bytes 3145744 | tf_op jit(solution)/shard_map/psum | solution.py:16
  203.9 4.4 fusion.9
  208.3 7.5 %all-to-all-start = ((f32[16,512,32]{1,2,0:T(8,128)}), f32[16,512,32]{1,2,0:T(8,128)}, u32[]{:S(2)}, u32[]{:S(2)}) async-start(f32[16,512,32]{1,2,0:T(8,128)} %bitcast.114), calls=%async_computation | async-start | bytes 2097152 | tf_op jit(solution)/shard_map/all_to_all | solution.py:43
  215.9 4.4 fusion.13
  220.3 22.1 %all-to-all-done = f32[16,512,32]{1,2,0:T(8,128)} async-done(((f32[16,512,32]{1,2,0:T(8,128)}), f32[16,512,32]{1,2,0:T(8,128)}, u32[]{:S(2)}, u32[]{:S(2)}) %all-to-all-start) | async-done | bytes 1048608 | tf_op jit(solution)/shard_map/all_to_all | solution.py:43
  242.4 5.0 %all-to-all-start.1 = ((f32[16,512,32]{1,2,0:T(8,128)}), f32[16,512,32]{1,2,0:T(8,128)}, u32[]{:S(2)}, u32[]{:S(2)}) async-start(f32[16,512,32]{1,2,0:T(8,128)} %bitcast.113), calls=%async_computation.1 | async-start | bytes 2097152 | tf_op jit(solution)/shard_map/all_to_all | solution.py:43
  250.2 23.7 %all-to-all-done.1 = f32[16,512,32]{1,2,0:T(8,128)} async-done(((f32[16,512,32]{1,2,0:T(8,128)}), f32[16,512,32]{1,2,0:T(8,128)}, u32[]{:S(2)}, u32[]{:S(2)}) %all-to-all-start.1) | async-done | bytes 1048608 | tf_op jit(solution)/shard_map/all_to_all | solution.py:43
  275.5 7.8 %all-to-all-start.7 = ((f32[32,512,32]{1,2,0:T(8,128)}), f32[32,512,32]{1,2,0:T(8,128)}, u32[]{:S(2)}, u32[]{:S(2)}) async-start(f32[32,512,32]{1,2,0:T(8,128)} %broadcast_in_dim.27), calls=%async_computation.7 | async-start | bytes 4194304 | tf_op jit(solution)/shard_map/all_to_all | solution.py:28
  285.4 42.1 %all-gather.5.cloned.1.call-done = f32[512,512]{0,1:T(8,128)} async-done(((f32[512,32]{0,1:T(8,128)}), f32[512,512]{0,1:T(8,128)}) %all-gather.5.cloned.1.call-update) | async-done | bytes 1048592 | tf_op jit(solution)/shard_map/all_gather | solution.py:119
  329.3 4.2 all-to-all-done.7
  343.0 7.9 %all-to-all-start.5 = ((f32[32,1,1024]{2,1,0:T(1,128)}), f32[32,1,1024]{2,1,0:T(1,128)S(1)}, u32[]{:S(2)}, u32[]{:S(2)}) async-start(f32[32,1,1024]{2,1,0:T(1,128)} %copy.30), calls=%async_computation.5 | async-start | bytes 262144 | tf_op jit(solution)/shard_map/all_to_all | solution.py:43
  350.9 4.4 fusion.17
  355.3 5.6 %all-to-all-done.5 = f32[32,1,1024]{2,1,0:T(1,128)S(1)} async-done(((f32[32,1,1024]{2,1,0:T(1,128)}), f32[32,1,1024]{2,1,0:T(1,128)S(1)}, u32[]{:S(2)}, u32[]{:S(2)}) %all-to-all-start.5) | async-done | bytes 131104 | tf_op jit(solution)/shard_map/all_to_all | solution.py:43
  360.9 4.3 all-to-all-start.3
  365.9 26.2 %all-to-all-done.3 = f32[16,512,32]{1,2,0:T(8,128)} async-done(((f32[16,512,32]{1,2,0:T(8,128)}), f32[16,512,32]{1,2,0:T(8,128)}, u32[]{:S(2)}, u32[]{:S(2)}) %all-to-all-start.3) | async-done | bytes 1048608 | tf_op jit(solution)/shard_map/all_to_all | solution.py:43
  392.2 16.4 %all_to_all.60 = f32[32,1,1024]{2,1,0:T(1,128)S(1)} all-to-all(f32[32,1,1024]{2,1,0:T(1,128)S(1)} %broadcast_in_dim.26), channel_id=1, replica_groups=mesh['row_0'=4,'row_1'=8,'col'=16] {'row_0','row_1'}, dimensions={0} | all-to-all | bytes 262144 | tf_op jit(solution)/shard_map/all_to_all | solution.py:28
  409.5 3.6 all-to-all-start.4
  419.8 6.4 %all-gather.7.cloned.1.call-done = f32[512,512]{0,1:T(8,128)} async-done(((f32[512,32]{0,1:T(8,128)}), f32[512,512]{0,1:T(8,128)}) %all-gather.7.cloned.1.call-update) | async-done | bytes 1048592 | tf_op jit(solution)/shard_map/all_gather | solution.py:119
  436.0 9.4 %all-to-all-start.8 = ((f32[32,1,1024]{2,1,0:T(1,128)}), f32[32,1,1024]{2,1,0:T(1,128)S(1)}, u32[]{:S(2)}, u32[]{:S(2)}) async-start(f32[32,1,1024]{2,1,0:T(1,128)} %copy.34), calls=%async_computation.8 | async-start | bytes 262144 | tf_op jit(solution)/shard_map/all_to_all | solution.py:43
  447.3 8.2 %all-to-all-done.8 = f32[32,1,1024]{2,1,0:T(1,128)S(1)} async-done(((f32[32,1,1024]{2,1,0:T(1,128)}), f32[32,1,1024]{2,1,0:T(1,128)S(1)}, u32[]{:S(2)}, u32[]{:S(2)}) %all-to-all-start.8) | async-done | bytes 131104 | tf_op jit(solution)/shard_map/all_to_all | solution.py:43
  456.3 4.4 all-to-all-start.9
  462.3 8.3 %all-to-all-done.9 = f32[32,1,1024]{2,1,0:T(1,128)S(1)} async-done(((f32[32,1,1024]{2,1,0:T(1,128)}), f32[32,1,1024]{2,1,0:T(1,128)S(1)}, u32[]{:S(2)}, u32[]{:S(2)}) %all-to-all-start.9) | async-done | bytes 131104 | tf_op jit(solution)/shard_map/all_to_all | solution.py:28
  (110 shorter events, 52.5 us)
Async XLA Ops:
  7.2 196.7 %copy-start = (f32[512,1024]{1,0:T(8,128)S(1)}, f32[512,1024]{1,0:T(8,128)}, u32[]{:S(2)}) copy-start(f32[512,1024]{1,0:T(8,128)} %param.5) | copy-start | bytes 6291460
  7.2 97.2 %all-reduce.7.cloned.1.call-start = ((), (), s32[]{:S(2)}) async-start(), calls=%async_computation.15 | async-start | bytes 6291456 | tf_op jit(solution)/shard_map/psum | solution.py:16
  13.2 91.2 %copy-start.14 = (bf16[2,32,512]{2,1,0:T(8,128)(2,1)S(1)}, bf16[2,32,512]{2,1,0:T(8,128)(2,1)}, u32[]{:S(2)}) copy-start(bf16[2,32,512]{2,1,0:T(8,128)(2,1)} %param.8) | copy-start | bytes 196612
  13.2 190.7 %all-reduce.5.cloned.1.call-start = ((), (), s32[]{:S(2)}) async-start(), calls=%async_computation.14 | async-start | bytes 6291456 | tf_op jit(solution)/shard_map/psum | solution.py:16
  105.9 102.4 %all-to-all-start.2 = ((bf16[16,32,512]{2,1,0:T(8,128)(2,1)}), bf16[16,32,512]{2,1,0:T(8,128)(2,1)S(1)}, u32[]{:S(2)}, u32[]{:S(2)}) async-start(bf16[16,32,512]{2,1,0:T(8,128)(2,1)} %broadcast_in_dim.24), calls=%async_computation.2 | async-start | bytes 1048576 | tf_op jit(solution)/shard_map/all_to_all | solution.py:28
  208.3 34.1 %all-to-all-start = ((f32[16,512,32]{1,2,0:T(8,128)}), f32[16,512,32]{1,2,0:T(8,128)}, u32[]{:S(2)}, u32[]{:S(2)}) async-start(f32[16,512,32]{1,2,0:T(8,128)} %bitcast.114), calls=%async_computation | async-start | bytes 2097152 | tf_op jit(solution)/shard_map/all_to_all | solution.py:43
  242.4 31.5 %all-to-all-start.1 = ((f32[16,512,32]{1,2,0:T(8,128)}), f32[16,512,32]{1,2,0:T(8,128)}, u32[]{:S(2)}, u32[]{:S(2)}) async-start(f32[16,512,32]{1,2,0:T(8,128)} %bitcast.113), calls=%async_computation.1 | async-start | bytes 2097152 | tf_op jit(solution)/shard_map/all_to_all | solution.py:43
  248.7 26.8 %copy-start.7 = (f32[512,32]{0,1:T(8,128)}, f32[512,32]{0,1:T(8,128)S(1)}, u32[]{:S(2)}) copy-start(f32[512,32]{0,1:T(8,128)S(1)} %reduce_sum.56) | copy-start | bytes 196612
  248.7 26.8 %copy-start.12 = (f32[512,32]{0,1:T(8,128)}, f32[512,32]{0,1:T(8,128)S(1)}, u32[]{:S(2)}) copy-start(f32[512,32]{0,1:T(8,128)S(1)} %negate_multiply_fusion) | copy-start | bytes 196612
  275.5 57.9 %all-to-all-start.7 = ((f32[32,512,32]{1,2,0:T(8,128)}), f32[32,512,32]{1,2,0:T(8,128)}, u32[]{:S(2)}, u32[]{:S(2)}) async-start(f32[32,512,32]{1,2,0:T(8,128)} %broadcast_in_dim.27), calls=%async_computation.7 | async-start | bytes 4194304 | tf_op jit(solution)/shard_map/all_to_all | solution.py:28
  283.3 44.2 %all-gather.5.cloned.1.call-start = ((), (), s32[]{:S(2)}) async-start(), calls=%async_computation.10 | async-start | bytes 1114112 | tf_op jit(solution)/shard_map/all_gather | solution.py:119
  284.1 132.1 %all-gather.9.cloned.1.call-start = ((), (), s32[]{:S(2)}) async-start(), calls=%async_computation.12 | async-start | bytes 1114112 | tf_op jit(solution)/shard_map/all_gather | solution.py:108
  343.0 17.9 %all-to-all-start.5 = ((f32[32,1,1024]{2,1,0:T(1,128)}), f32[32,1,1024]{2,1,0:T(1,128)S(1)}, u32[]{:S(2)}, u32[]{:S(2)}) async-start(f32[32,1,1024]{2,1,0:T(1,128)} %copy.30), calls=%async_computation.5 | async-start | bytes 262144 | tf_op jit(solution)/shard_map/all_to_all | solution.py:43
  355.3 53.3 %copy-start.13 = (bf16[32,512]{1,0:T(8,128)(2,1)S(1)}, bf16[32,512]{1,0:T(8,128)(2,1)}, u32[]{:S(2)}) copy-start(bf16[32,512]{1,0:T(8,128)(2,1)} %get-tuple-element.29) | copy-start | bytes 98308
  360.9 31.2 %all-to-all-start.3 = ((f32[16,512,32]{1,2,0:T(8,128)}), f32[16,512,32]{1,2,0:T(8,128)}, u32[]{:S(2)}, u32[]{:S(2)}) async-start(f32[16,512,32]{1,2,0:T(8,128)} %bitcast.112), calls=%async_computation.3 | async-start | bytes 2097152 | tf_op jit(solution)/shard_map/all_to_all | solution.py:43
  365.2 60.9 %all-gather.7.cloned.1.call-start = ((), (), s32[]{:S(2)}) async-start(), calls=%async_computation.11 | async-start | bytes 1114112 | tf_op jit(solution)/shard_map/all_gather | solution.py:119
  409.5 20.1 %all-to-all-start.4 = ((bf16[16,32,512]{2,1,0:T(8,128)(2,1)}), bf16[16,32,512]{2,1,0:T(8,128)(2,1)S(1)}, u32[]{:S(2)}, u32[]{:S(2)}) async-start(bf16[16,32,512]{2,1,0:T(8,128)(2,1)} %broadcast_in_dim.25), calls=%async_computation.4 | async-start | bytes 1048576 | tf_op jit(solution)/shard_map/all_to_all | solution.py:28
  413.1 58.3 %all-gather.11.cloned.1.call-start = ((), (), s32[]{:S(2)}) async-start(), calls=%async_computation.13 | async-start | bytes 1114112 | tf_op jit(solution)/shard_map/all_gather | solution.py:108
  431.4 29.3 %copy-start.4 = (f32[512,32]{0,1:T(8,128)S(1)}, f32[512,32]{0,1:T(8,128)}, u32[]{:S(2)}) copy-start(f32[512,32]{0,1:T(8,128)} %copy-done.3) | copy-start | bytes 196612
  433.3 27.4 %copy-start.9 = (f32[512,32]{0,1:T(8,128)S(1)}, f32[512,32]{0,1:T(8,128)}, u32[]{:S(2)}) copy-start(f32[512,32]{0,1:T(8,128)} %copy-done.8) | copy-start | bytes 196612
  434.3 37.0 %copy-start.6 = (f32[512,32]{0,1:T(8,128)S(1)}, f32[512,32]{0,1:T(8,128)}, u32[]{:S(2)}) copy-start(f32[512,32]{0,1:T(8,128)} %copy-done.5) | copy-start | bytes 196612
  436.0 19.5 %all-to-all-start.8 = ((f32[32,1,1024]{2,1,0:T(1,128)}), f32[32,1,1024]{2,1,0:T(1,128)S(1)}, u32[]{:S(2)}, u32[]{:S(2)}) async-start(f32[32,1,1024]{2,1,0:T(1,128)} %copy.34), calls=%async_computation.8 | async-start | bytes 262144 | tf_op jit(solution)/shard_map/all_to_all | solution.py:43
  456.3 14.2 %all-to-all-start.9 = ((f32[32,1,1024]{2,1,0:T(1,128)}), f32[32,1,1024]{2,1,0:T(1,128)S(1)}, u32[]{:S(2)}, u32[]{:S(2)}) async-start(f32[32,1,1024]{2,1,0:T(1,128)} %broadcast_in_dim.28), calls=%async_computation.9 | async-start | bytes 262144 | tf_op jit(solution)/shard_map/all_to_all | solution.py:28
  462.3 12.8 %copy-start.10 = (f32[512,32]{0,1:T(8,128)S(1)}, f32[512,32]{0,1:T(8,128)}, u32[]{:S(2)}) copy-start(f32[512,32]{0,1:T(8,128)} %fusion.6) | copy-start | bytes 196612
  (6 other events, 34.3 us)
Sparse Core Ops, SparseCore 0:
  13.3 91.0 all-reduce.6
  107.1 96.7 all-reduce.4
  286.8 40.6 all-gather.4
  336.8 38.3 all-gather.8
  377.7 48.4 all-gather.6
  428.1 40.9 all-gather.10
where the time goes:
time: 484 us; the launch traced here: 483 us
  waiting for transfers between devices  331 us (68%)
  starting transfers between devices  57.7 us (12%)
  matrix products  32.3 us (7%)
  other arithmetic  17.6 us (4%)
  blocking collectives  16.4 us (3%)
  between operations  14.5 us (3%)
  local copies, waits for them, and re-layouts  12.9 us (3%)
    psum x2, waiting for transfers between devices, from_root(): array = lax.psum(array, axis)  182 us
    all_to_all x5, waiting for transfers between devices, sent_and_summed(): lax.all_to_all(blocks, axis, split_axis=0, concat_axis=0, tiled=True)  85.8 us
    all_gather x2, waiting for transfers between devices, local(): current_full = lax.all_gather(current, 'col', axis=1, tiled=True)  48.5 us
    all_to_all x5, starting transfers between devices, sent_and_summed(): lax.all_to_all(blocks, axis, split_axis=0, concat_axis=0, tiled=True)  34.2 us
    dot_general x16, matrix products, product(): jnp.dot(left, right, precision=precise, preferred_element_type=jnp.float32)  32.3 us
    all_to_all x4, starting transfers between devices, copy_for_each(): return lax.all_to_all(copies, axis, split_axis=0, concat_axis=0, tiled=True)  23.2 us
    all_to_all x1, blocking collectives, copy_for_each(): return lax.all_to_all(copies, axis, split_axis=0, concat_axis=0, tiled=True)  16.4 us
    all_to_all x4, waiting for transfers between devices, copy_for_each(): return lax.all_to_all(copies, axis, split_axis=0, concat_axis=0, tiled=True)  13.9 us
  transfers between devices with their start and end apart: 15, of which 12 were waited for; matrix products, arithmetic and copies ran while one was open for 10% of the time, Pallas kernels for 0%

commit v1 on v0

--- a/solution.py
+++ b/solution.py
@@ -13,7 +13,7 @@
 def from_root(array, axes, root):
     array = jnp.where(lax.axis_index(axes) == root, array, jnp.zeros_like(array))
     for axis in axes:
-        array = lax.psum(array, axis)
+        array = jnp.sum(lax.all_gather(array, axis), axis=0)
     return array
 
 

time: 484 us -> 819 us (1.69)
  waiting for transfers between devices: 331 us -> 620 us
  other arithmetic: 17.6 us -> 58.2 us
    all_gather x0 -> x12, waiting for transfers between devices: none -> 496 us  [from_root(): array = jnp.sum(lax.all_gather(array, axis), axis=0)]
    psum x2 -> x0, waiting for transfers between devices: 182 us -> none  [from_root(): array = lax.psum(array, axis)]
    reduce_sum x0 -> x12, other arithmetic: none -> 38.3 us  [from_root(): array = jnp.sum(lax.all_gather(array, axis), axis=0)]
    all_to_all x5, waiting for transfers between devices: 85.8 us -> 64.1 us  [sent_and_summed(): lax.all_to_all(blocks, axis, split_axis=0, concat_axis=0, tiled=True)]
    all_gather x2, waiting for transfers between devices: 48.5 us -> 40 us  [local(): current_full = lax.all_gather(current, 'col', axis=1, tiled=True)]
  transfers between devices with their start and end apart: 15 -> 25, of which waited for: 12 -> 19; matrix products, arithmetic and copies ran while one was open for 10% -> 12% of each run, Pallas kernels for 0% -> 0%
where the time goes in v1:
time: 819 us; the launch traced here: 816 us
  waiting for transfers between devices  620 us (76%)
  starting transfers between devices  59.6 us (7%)
  other arithmetic  58.2 us (7%)
  matrix products  32.7 us (4%)
  blocking collectives  15.6 us (2%)
  local copies, waits for them, and re-layouts  15.3 us (2%)
  between operations  14.4 us (2%)
    all_gather x12, waiting for transfers between devices, from_root(): array = jnp.sum(lax.all_gather(array, axis), axis=0)  496 us
    all_to_all x5, waiting for transfers between devices, sent_and_summed(): lax.all_to_all(blocks, axis, split_axis=0, concat_axis=0, tiled=True)  64.1 us
    all_gather x2, waiting for transfers between devices, local(): current_full = lax.all_gather(current, 'col', axis=1, tiled=True)  40 us
    reduce_sum x12, other arithmetic, from_root(): array = jnp.sum(lax.all_gather(array, axis), axis=0)  38.3 us
    all_to_all x5, starting transfers between devices, sent_and_summed(): lax.all_to_all(blocks, axis, split_axis=0, concat_axis=0, tiled=True)  34.1 us
    dot_general x16, matrix products, product(): jnp.dot(left, right, precision=precise, preferred_element_type=jnp.float32)  32.7 us
    all_to_all x4, starting transfers between devices, copy_for_each(): return lax.all_to_all(copies, axis, split_axis=0, concat_axis=0, tiled=True)  24.9 us
  transfers between devices with their start and end apart: 25, of which 19 were waited for; matrix products, arithmetic and copies ran while one was open for 12% of the time, Pallas kernels for 0%

profile of v1, /device:TPU:8, one launch (start us, length us, event | category | flops | bytes accessed | tf_op | source)
XLA Modules:
  0.0 816.1 jit_solution(10404926164793665126)
XLA Ops:
  14.9 37.5 %all-gather.25.cloned.1.call-done = bf16[4,512,512]{2,1,0:T(8,128)(2,1)} async-done(((bf16[1,512,512]{2,1,0:T(8,128)(2,1)}), bf16[4,512,512]{2,1,0:T(8,128)(2,1)}) %all-gather.25.cloned.1.call-update) | async-done | bytes 2097168 | tf_op jit(solution)/shard_map/all_gather | solution.py:16
  55.4 35.4 %all-gather.23.cloned.1.call-done = bf16[4,512,512]{2,1,0:T(8,128)(2,1)} async-done(((bf16[1,512,512]{2,1,0:T(8,128)(2,1)}), bf16[4,512,512]{2,1,0:T(8,128)(2,1)}) %all-gather.23.cloned.1.call-update) | async-done | bytes 2097168 | tf_op jit(solution)/shard_map/all_gather | solution.py:16
  93.7 35.4 %all-gather.29.cloned.1.call-done = bf16[4,512,512]{2,1,0:T(8,128)(2,1)} async-done(((bf16[1,512,512]{2,1,0:T(8,128)(2,1)}), bf16[4,512,512]{2,1,0:T(8,128)(2,1)}) %all-gather.29.cloned.1.call-update) | async-done | bytes 2097168 | tf_op jit(solution)/shard_map/all_gather | solution.py:16
  132.1 35.2 %all-gather.27.cloned.1.call-done = bf16[4,512,512]{2,1,0:T(8,128)(2,1)} async-done(((bf16[1,512,512]{2,1,0:T(8,128)(2,1)}), bf16[4,512,512]{2,1,0:T(8,128)(2,1)}) %all-gather.27.cloned.1.call-update) | async-done | bytes 2097168 | tf_op jit(solution)/shard_map/all_gather | solution.py:16
  170.2 35.2 %all-gather.35.cloned.1.call-done = bf16[4,512,512]{2,1,0:T(8,128)(2,1)} async-done(((bf16[1,512,512]{2,1,0:T(8,128)(2,1)}), bf16[4,512,512]{2,1,0:T(8,128)(2,1)}) %all-gather.35.cloned.1.call-update) | async-done | bytes 2097168 | tf_op jit(solution)/shard_map/all_gather | solution.py:16
  208.4 35.2 %all-gather.33.cloned.1.call-done = bf16[4,512,512]{2,1,0:T(8,128)(2,1)} async-done(((bf16[1,512,512]{2,1,0:T(8,128)(2,1)}), bf16[4,512,512]{2,1,0:T(8,128)(2,1)}) %all-gather.33.cloned.1.call-update) | async-done | bytes 2097168 | tf_op jit(solution)/shard_map/all_gather | solution.py:16
  248.0 7.5 all-to-all-start.2
  255.5 46.0 %all-gather.45.cloned.1.call-done = bf16[4096,512]{1,0:T(8,128)(2,1)} async-done(((bf16[512,512]{1,0:T(8,128)(2,1)}), bf16[4096,512]{1,0:T(8,128)(2,1)}) %all-gather.45.cloned.1.call-update) | async-done | bytes 4194320 | tf_op jit(solution)/shard_map/all_gather | solution.py:16
  304.5 55.2 %all-gather.43.cloned.1.call-done = bf16[4096,512]{1,0:T(8,128)(2,1)} async-done(((bf16[512,512]{1,0:T(8,128)(2,1)}), bf16[4096,512]{1,0:T(8,128)(2,1)}) %all-gather.43.cloned.1.call-update) | async-done | bytes 4194320 | tf_op jit(solution)/shard_map/all_gather | solution.py:16
  367.8 7.5 all-to-all-start
  375.3 42.6 %all-gather.49.cloned.1.call-done = bf16[4096,512]{1,0:T(8,128)(2,1)} async-done(((bf16[512,512]{1,0:T(8,128)(2,1)}), bf16[4096,512]{1,0:T(8,128)(2,1)}) %all-gather.49.cloned.1.call-update) | async-done | bytes 4194320 | tf_op jit(solution)/shard_map/all_gather | solution.py:16
  421.0 55.0 %all-gather.47.cloned.1.call-done = bf16[4096,512]{1,0:T(8,128)(2,1)} async-done(((bf16[512,512]{1,0:T(8,128)(2,1)}), bf16[4096,512]{1,0:T(8,128)(2,1)}) %all-gather.47.cloned.1.call-update) | async-done | bytes 4194320 | tf_op jit(solution)/shard_map/all_gather | solution.py:16
  484.0 7.5 all-to-all-start.1
  494.4 23.7 %all-to-all-done.1 = f32[16,512,32]{1,2,0:T(8,128)} async-done(((f32[16,512,32]{1,2,0:T(8,128)}), f32[16,512,32]{1,2,0:T(8,128)}, u32[]{:S(2)}, u32[]{:S(2)}) %all-to-all-start.1) | async-done | bytes 1048608 | tf_op jit(solution)/shard_map/all_to_all | solution.py:43
  519.7 9.0 %all-to-all-start.7 = ((f32[32,512,32]{1,2,0:T(8,128)}), f32[32,512,32]{1,2,0:T(8,128)}, u32[]{:S(2)}, u32[]{:S(2)}) async-start(f32[32,512,32]{1,2,0:T(8,128)} %broadcast_in_dim.27), calls=%async_computation.7 | async-start | bytes 4194304 | tf_op jit(solution)/shard_map/all_to_all | solution.py:28
  531.7 7.8 all-gather.53.cloned.1.call-done
  543.3 75.2 %all-gather.51.cloned.1.call-done = bf16[4096,512]{1,0:T(8,128)(2,1)} async-done(((bf16[512,512]{1,0:T(8,128)(2,1)}), bf16[4096,512]{1,0:T(8,128)(2,1)}) %all-gather.51.cloned.1.call-update) | async-done | bytes 4194320 | tf_op jit(solution)/shard_map/all_gather | solution.py:16
  623.5 40.0 %all-gather.31.cloned.1.call-done = f32[512,512]{0,1:T(8,128)} async-done(((f32[512,32]{0,1:T(8,128)}), f32[512,512]{0,1:T(8,128)}) %all-gather.31.cloned.1.call-update) | async-done | bytes 1048592 | tf_op jit(solution)/shard_map/all_gather | solution.py:119
  679.5 9.8 %all-to-all-start.5 = ((f32[32,1,1024]{2,1,0:T(1,128)}), f32[32,1,1024]{2,1,0:T(1,128)S(1)}, u32[]{:S(2)}, u32[]{:S(2)}) async-start(f32[32,1,1024]{2,1,0:T(1,128)} %copy.30), calls=%async_computation.5 | async-start | bytes 262144 | tf_op jit(solution)/shard_map/all_to_all | solution.py:43
  704.7 25.9 %all-to-all-done.3 = f32[16,512,32]{1,2,0:T(8,128)} async-done(((f32[16,512,32]{1,2,0:T(8,128)}), f32[16,512,32]{1,2,0:T(8,128)}, u32[]{:S(2)}, u32[]{:S(2)}) %all-to-all-start.3) | async-done | bytes 1048608 | tf_op jit(solution)/shard_map/all_to_all | solution.py:43
  730.7 15.6 %all_to_all.60 = f32[32,1,1024]{2,1,0:T(1,128)S(1)} all-to-all(f32[32,1,1024]{2,1,0:T(1,128)S(1)} %broadcast_in_dim.26), channel_id=1, replica_groups=mesh['row_0'=4,'row_1'=8,'col'=16] {'row_0','row_1'}, dimensions={0} | all-to-all | bytes 262144 | tf_op jit(solution)/shard_map/all_to_all | solution.py:28
  759.8 7.1 all-to-all-done.4
  779.8 8.7 %all-to-all-done.8 = f32[32,1,1024]{2,1,0:T(1,128)S(1)} async-done(((f32[32,1,1024]{2,1,0:T(1,128)}), f32[32,1,1024]{2,1,0:T(1,128)S(1)}, u32[]{:S(2)}, u32[]{:S(2)}) %all-to-all-start.8) | async-done | bytes 131104 | tf_op jit(solution)/shard_map/all_to_all | solution.py:43
  795.5 8.9 %all-to-all-done.9 = f32[32,1,1024]{2,1,0:T(1,128)S(1)} async-done(((f32[32,1,1024]{2,1,0:T(1,128)}), f32[32,1,1024]{2,1,0:T(1,128)S(1)}, u32[]{:S(2)}, u32[]{:S(2)}) %all-to-all-start.9) | async-done | bytes 131104 | tf_op jit(solution)/shard_map/all_to_all | solution.py:28
  (152 shorter events, 134.6 us)
Async XLA Ops:
  7.2 45.3 %all-gather.25.cloned.1.call-start = ((), (), s32[]{:S(2)}) async-start(), calls=%async_computation.11 | async-start | bytes 2621440 | tf_op jit(solution)/shard_map/all_gather | solution.py:16
  11.7 79.1 %all-gather.23.cloned.1.call-start = ((), (), s32[]{:S(2)}) async-start(), calls=%async_computation.10 | async-start | bytes 2621440 | tf_op jit(solution)/shard_map/all_gather | solution.py:16
  12.4 116.7 %all-gather.29.cloned.1.call-start = ((), (), s32[]{:S(2)}) async-start(), calls=%async_computation.13 | async-start | bytes 2621440 | tf_op jit(solution)/shard_map/all_gather | solution.py:16
  13.2 154.1 %all-gather.27.cloned.1.call-start = ((), (), s32[]{:S(2)}) async-start(), calls=%async_computation.12 | async-start | bytes 2621440 | tf_op jit(solution)/shard_map/all_gather | solution.py:16
  13.7 191.7 %all-gather.35.cloned.1.call-start = ((), (), s32[]{:S(2)}) async-start(), calls=%async_computation.16 | async-start | bytes 2621440 | tf_op jit(solution)/shard_map/all_gather | solution.py:16
  14.3 229.3 %all-gather.33.cloned.1.call-start = ((), (), s32[]{:S(2)}) async-start(), calls=%async_computation.15 | async-start | bytes 2621440 | tf_op jit(solution)/shard_map/all_gather | solution.py:16
  14.9 286.6 %all-gather.45.cloned.1.call-start = ((), (), s32[]{:S(2)}) async-start(), calls=%async_computation.21 | async-start | bytes 4718592 | tf_op jit(solution)/shard_map/all_gather | solution.py:16
  55.4 304.3 %all-gather.43.cloned.1.call-start = ((), (), s32[]{:S(2)}) async-start(), calls=%async_computation.20 | async-start | bytes 4718592 | tf_op jit(solution)/shard_map/all_gather | solution.py:16
  93.7 324.2 %all-gather.49.cloned.1.call-start = ((), (), s32[]{:S(2)}) async-start(), calls=%async_computation.23 | async-start | bytes 4718592 | tf_op jit(solution)/shard_map/all_gather | solution.py:16
  132.0 344.0 %all-gather.47.cloned.1.call-start = ((), (), s32[]{:S(2)}) async-start(), calls=%async_computation.22 | async-start | bytes 4718592 | tf_op jit(solution)/shard_map/all_gather | solution.py:16
  170.2 369.4 %all-gather.53.cloned.1.call-start = ((), (), s32[]{:S(2)}) async-start(), calls=%async_computation.25 | async-start | bytes 4718592 | tf_op jit(solution)/shard_map/all_gather | solution.py:16
  208.4 410.1 %all-gather.51.cloned.1.call-start = ((), (), s32[]{:S(2)}) async-start(), calls=%async_computation.24 | async-start | bytes 4718592 | tf_op jit(solution)/shard_map/all_gather | solution.py:16
  248.0 119.8 %all-to-all-start.2 = ((bf16[16,32,512]{2,1,0:T(8,128)(2,1)}), bf16[16,32,512]{2,1,0:T(8,128)(2,1)S(1)}, u32[]{:S(2)}, u32[]{:S(2)}) async-start(bf16[16,32,512]{2,1,0:T(8,128)(2,1)} %broadcast_in_dim.24), calls=%async_computation.2 | async-start | bytes 1048576 | tf_op jit(solution)/shard_map/all_to_all | solution.py:28
  367.8 116.3 %all-to-all-start = ((f32[16,512,32]{1,2,0:T(8,128)}), f32[16,512,32]{1,2,0:T(8,128)}, u32[]{:S(2)}, u32[]{:S(2)}) async-start(f32[16,512,32]{1,2,0:T(8,128)} %bitcast.118), calls=%async_computation | async-start | bytes 2097152 | tf_op jit(solution)/shard_map/all_to_all | solution.py:43
  484.0 34.1 %all-to-all-start.1 = ((f32[16,512,32]{1,2,0:T(8,128)}), f32[16,512,32]{1,2,0:T(8,128)}, u32[]{:S(2)}, u32[]{:S(2)}) async-start(f32[16,512,32]{1,2,0:T(8,128)} %bitcast.120), calls=%async_computation.1 | async-start | bytes 2097152 | tf_op jit(solution)/shard_map/all_to_all | solution.py:43
  519.7 145.6 %all-to-all-start.7 = ((f32[32,512,32]{1,2,0:T(8,128)}), f32[32,512,32]{1,2,0:T(8,128)}, u32[]{:S(2)}, u32[]{:S(2)}) async-start(f32[32,512,32]{1,2,0:T(8,128)} %broadcast_in_dim.27), calls=%async_computation.7 | async-start | bytes 4194304 | tf_op jit(solution)/shard_map/all_to_all | solution.py:28
  528.8 134.8 %all-gather.31.cloned.1.call-start = ((), (), s32[]{:S(2)}) async-start(), calls=%async_computation.14 | async-start | bytes 1114112 | tf_op jit(solution)/shard_map/all_gather | solution.py:119
  529.5 224.5 %all-gather.39.cloned.1.call-start = ((), (), s32[]{:S(2)}) async-start(), calls=%async_computation.18 | async-start | bytes 1114112 | tf_op jit(solution)/shard_map/all_gather | solution.py:108
  679.5 19.9 %all-to-all-start.5 = ((f32[32,1,1024]{2,1,0:T(1,128)}), f32[32,1,1024]{2,1,0:T(1,128)S(1)}, u32[]{:S(2)}, u32[]{:S(2)}) async-start(f32[32,1,1024]{2,1,0:T(1,128)} %copy.30), calls=%async_computation.5 | async-start | bytes 262144 | tf_op jit(solution)/shard_map/all_to_all | solution.py:43
  699.4 31.1 %all-to-all-start.3 = ((f32[16,512,32]{1,2,0:T(8,128)}), f32[16,512,32]{1,2,0:T(8,128)}, u32[]{:S(2)}, u32[]{:S(2)}) async-start(f32[16,512,32]{1,2,0:T(8,128)} %bitcast.119), calls=%async_computation.3 | async-start | bytes 2097152 | tf_op jit(solution)/shard_map/all_to_all | solution.py:43
  704.0 53.7 %all-gather.37.cloned.1.call-start = ((), (), s32[]{:S(2)}) async-start(), calls=%async_computation.17 | async-start | bytes 1114112 | tf_op jit(solution)/shard_map/all_gather | solution.py:119
  747.1 19.8 %all-to-all-start.4 = ((bf16[16,32,512]{2,1,0:T(8,128)(2,1)}), bf16[16,32,512]{2,1,0:T(8,128)(2,1)S(1)}, u32[]{:S(2)}, u32[]{:S(2)}) async-start(bf16[16,32,512]{2,1,0:T(8,128)(2,1)} %broadcast_in_dim.25), calls=%async_computation.4 | async-start | bytes 1048576 | tf_op jit(solution)/shard_map/all_to_all | solution.py:28
  751.0 54.2 %all-gather.41.cloned.1.call-start = ((), (), s32[]{:S(2)}) async-start(), calls=%async_computation.19 | async-start | bytes 1114112 | tf_op jit(solution)/shard_map/all_gather | solution.py:108
  773.3 15.3 %all-to-all-start.8 = ((f32[32,1,1024]{2,1,0:T(1,128)}), f32[32,1,1024]{2,1,0:T(1,128)S(1)}, u32[]{:S(2)}, u32[]{:S(2)}) async-start(f32[32,1,1024]{2,1,0:T(1,128)} %copy.34), calls=%async_computation.8 | async-start | bytes 262144 | tf_op jit(solution)/shard_map/all_to_all | solution.py:43
  (16 other events, 656.2 us)
Sparse Core Ops, SparseCore 0:
  11.8 40.6 all-gather.24
  54.6 36.1 all-gather.22
  92.9 36.1 all-gather.28
  131.1 36.1 all-gather.26
  169.2 36.1 all-gather.34
  207.4 36.1 all-gather.32
  245.7 55.7 all-gather.44
  303.6 56.0 all-gather.42
  361.8 56.0 all-gather.48
  419.8 56.0 all-gather.46
  478.1 61.4 all-gather.52
  541.5 76.9 all-gather.50
  621.2 42.3 all-gather.30
  668.7 39.9 all-gather.38
  711.2 42.7 all-gather.36
  757.8 38.9 all-gather.40
